TPU v7x, 32 devices: a whole 2x2x4 slice. The times are simulated.
32 devices in a mesh: rep: 2 (over x), mp: 16 (over z, y, core).
Axes of the slice: x: 2, y: 2, z: 4, core: 2. Of those that a mesh axis runs over, the one named last changes fastest.
Arguments:
- tokens: bfloat16 [1280, 3072], P(('rep', 'mp')), may hold values from -6 to 6
- w_in: bfloat16 [2, 3072, 2, 12288], P('rep', None, None, 'mp'), may hold values from -0.109375 to 0.109375
- w_down: bfloat16 [2, 12288, 3072], P('rep', 'mp'), may hold values from -0.0546875 to 0.0546875
- norm_gain: float32 [3072], replicated, may hold values from 0.1 to 1.9
- final_gain: float32 [3072], replicated, may hold values from 0.1 to 1.9
- value_head: float32 [3072], replicated, may hold values from -0.6 to 0.6
- owner: int32 [16], P('mp'), may hold values from 0 to 1
- lengths: int32 [16], P('rep'), may hold values from 20 to 80, as said below
- offsets: int32 [16], P('rep'), may hold values from 0 to 620, as said below
Outputs:
- mixed: bfloat16 [1280, 3072], P(('rep', 'mp'))
- rewards: float32 [16], P('rep')
Inputs may be any that keep to these rules, and one draw needn't show every extreme that they name: `lengths`: every rollout is at least a quarter of 80 long; in each group one rollout has exactly 80 tokens. `offsets`: rollout j of a group lies wholly within slots j * 80 to (j + 1) * 80 - 1 of its group; the other slots are padding.
All inputs are finite; a program needn't handle non-finite values.
Results may differ from a plain program's by a relative error of at most 0.0046.
Values may be sent and summed in bfloat16 or wider, within the bound.
A program may use at most 128 MiB of HBM per device.

v0:
```python
import jax
import jax.numpy as jnp
from jax import lax
from jax.sharding import PartitionSpec as P


def spread(value, axis, source):
    kept = jnp.where(lax.axis_index(axis) == source, value, 0).astype(value.dtype)
    return lax.psum(kept, axis)


def membership(slots, lengths, offsets):
    inside = (slots[:, None] >= offsets[None, :]) & (
        slots[:, None] < offsets[None, :] + lengths[None, :]
    )
    return inside.astype(jnp.float32)


def per_device(tokens, w_in, w_down, norm_gain, final_gain, value_head, owner, lengths, offsets):
    owner_index = owner[0]
    tok_rows = tokens.shape[0]
    width = tokens.shape[1]
    hidden_cols = w_in.shape[3]
    tokens_f = tokens.astype(jnp.float32)
    normed = (
        tokens_f
        * lax.rsqrt(jnp.mean(tokens_f * tokens_f, axis=1, keepdims=True) + 1e-06)
        * norm_gain
    ).astype(jnp.bfloat16)
    inner_local, outer_local = (
        spread(w_in, "rep", owner_index),
        spread(w_down, "rep", owner_index),
    )
    inner_matrix = inner_local.reshape(width, 2 * hidden_cols)
    piece = lax.all_gather(normed, "mp", axis=0, tiled=True)
    slots = jnp.arange(piece.shape[0], dtype=jnp.int32)
    row_count = piece.shape[0]
    products = jnp.dot(piece, inner_matrix, preferred_element_type=jnp.float32).reshape(
        row_count, 2, hidden_cols
    )
    gate_part = products[:, 0, :]
    up_part = products[:, 1, :]
    hidden = (
        jax.nn.gelu(gate_part, approximate=True)
        * up_part
        * jnp.sum(membership(slots, lengths, offsets), axis=1)[:, None]
    ).astype(jnp.bfloat16)
    outer_matrix = outer_local.reshape(hidden_cols, width)
    delta = lax.psum_scatter(
        jnp.dot(hidden, outer_matrix, preferred_element_type=jnp.float32),
        "mp",
        scatter_dimension=0,
        tiled=True,
    )
    resid = tokens_f + delta
    mixed = resid.astype(jnp.bfloat16)
    final = resid * lax.rsqrt(jnp.mean(resid * resid, axis=1, keepdims=True) + 1e-06) * final_gain
    values = jnp.dot(final, value_head, precision=lax.Precision.HIGHEST)
    own_slots = lax.axis_index("mp") * tok_rows + jnp.arange(tok_rows, dtype=jnp.int32)
    member = membership(own_slots, lengths, offsets)
    partial_sums = jnp.dot(values, member, precision=lax.Precision.HIGHEST)
    totals = lax.psum(partial_sums, "mp")
    rewards = totals / lengths.astype(jnp.float32)
    return (mixed, rewards)


def solution(mesh):
    in_specs = (
        P(("rep", "mp"), None),
        P("rep", None, None, "mp"),
        P("rep", "mp", None),
        P(),
        P(),
        P(),
        P("mp"),
        P("rep"),
        P("rep"),
    )
    out_specs = (P(("rep", "mp"), None), P("rep"))
    return jax.shard_map(
        per_device, mesh=mesh, in_specs=in_specs, out_specs=out_specs, check_vma=False
    )
```

profile of v0, /device:TPU:0, one launch (start us, length us, event | category | flops | bytes accessed | tf_op | source)
XLA Modules:
  0.0 530.3 jit_solution(2742017542717599871)
XLA Ops:
  8.0 0.0 copy-start
  8.0 0.0 all-gather.2.cloned.1.call-start
  8.1 1.1 fusion.19
  9.2 1.8 fusion.21
  10.9 0.0 all-gather.2.cloned.1.call-update
  11.0 0.0 all-reduce.3.cloned.1.call-start
  11.7 9.3 %broadcast_select_fusion = bf16[1,3072,2,768]{3,2,1,0:T(2,128)(2,1)} fusion(bf16[1,3072,2,768]{3,2,1,0:T(2,128)(2,1)} %param.10, pred[]{:T(512)S(6)} %eq.4), kind=kLoop, calls=%fused_computation | loop fusion | flops 4718592 | bytes 18874368 | tf_op jit(solution)/shard_map/jit(_where)/select_n | solution.py:8
  20.9 23.8 %copy.13 = bf16[1,3072,2,768]{1,3,2,0:T(8,128)(2,1)} copy(bf16[1,3072,2,768]{3,2,1,0:T(2,128)(2,1)} %broadcast_select_fusion) | data formatting | bytes 18874368 | tf_op jit(solution)/shard_map/reshape | solution.py:34
  44.7 2.6 select_bitcast_fusion
  47.3 0.0 copy-start.3
  47.3 0.0 copy-start.5
  47.3 0.0 all-reduce.3.cloned.1.call-update
  47.3 0.0 reduce-scatter.2.cloned.1.call-start
  47.4 0.6 copy-done.3
  47.9 0.0 copy-done.5
  48.0 0.1 convert_reduce_fusion
  48.1 15.4 %all-gather.2.cloned.1.call-done = bf16[640,3072]{1,0:T(8,128)(2,1)} async-done(((bf16[40,3072]{1,0:T(8,128)(2,1)}), bf16[640,3072]{1,0:T(8,128)(2,1)}) %all-gather.2.cloned.1.call-update) | async-done | bytes 3932176 | tf_op jit(solution)/shard_map/all_gather | solution.py:35
  63.5 311.1 %all-reduce.3.cloned.1.call-done = (bf16[768,3072]{1,0:T(8,128)(2,1)}, bf16[2,768,3072]{2,1,0:T(8,128)(2,1)}) async-done(((bf16[768,3072]{1,0:T(8,128)(2,1)}, bf16[2,768,3072]{2,1,0:T(8,128)(2,1)}), (bf16[768,3072]{1,0:T(8,128)(2,1)}, bf16[2,768,3072]{2,1,0:T(8,128)(2,1)})) %all-reduce.3.cloned.1.call-update) | async-done | bytes 14155792 | tf_op jit(solution)/shard_map/psum | solution.py:9
  374.6 0.0 copy-start.4
  374.6 10.2 %fusion = f32[640,2,768]{2,0,1:T(8,128)S(1)} fusion(bf16[2,768,3072]{2,1,0:T(8,128)(2,1)} %get-tuple-element.3, bf16[640,3072]{1,0:T(8,128)(2,1)} %all-gather.2.cloned.1.call-done), kind=kOutput, calls=%fused_computation.2 | convolution fusion | flops 6039797760 | bytes 17301504 | tf_op jit(solution)/shard_map/dot_general | solution.py:38
  384.8 0.0 copy-done.4
  384.8 6.4 %fusion.12 = f32[640,3072]{1,0:T(8,128)} fusion(bf16[768,3072]{1,0:T(8,128)(2,1)S(1)} %copy-done.4, f32[640,2,768]{2,0,1:T(8,128)S(1)} %fusion, f32[640]{0:T(1024)S(1)} %convert_reduce_fusion), kind=kOutput, calls=%fused_computation.17 | convolution fusion | flops 3025305600 | bytes 16517632 | tf_op jit(solution)/shard_map/dot_general | solution.py:50
  391.1 0.0 copy-start.1
  391.1 0.0 copy-start.2
  391.1 0.0 reduce-scatter.2.cloned.1.call-update
  391.2 95.3 %reduce-scatter.2.cloned.1.call-done = f32[40,3072]{1,0:T(8,128)} async-done(((f32[640,3072]{1,0:T(8,128)}), f32[40,3072]{1,0:T(8,128)}) %reduce-scatter.2.cloned.1.call-update) | async-done | bytes 491536 | tf_op jit(solution)/shard_map/reduce_scatter | solution.py:49
  486.5 0.0 copy-done.1
  486.5 1.9 multiply_reduce_fusion
  488.4 0.0 copy-done
  488.4 0.0 copy-done.2
  488.4 1.6 convolution_bitcast_fusion.1
  490.1 0.2 convolution_bitcast_fusion
  490.3 32.1 %psum.23 = f32[8]{0:T(128)S(1)} all-reduce(f32[8]{0:T(128)S(1)} %convolution_bitcast_fusion), channel_id=1, replica_groups=mesh['rep'=2,'mp'=16] {'mp'}, use_global_device_ids=true, to_apply=%region_6.7 | all-reduce | flops 8 | bytes 64 | tf_op jit(solution)/shard_map/psum | solution.py:62
  522.3 0.5 convert_divide_fusion
  (4 shorter events, 0.0 us)
Async XLA Ops:
  8.0 480.4 %copy-start = (f32[3072]{0:T(1024)S(1)}, f32[3072]{0:T(1024)}, u32[]{:S(2)}) copy-start(f32[3072]{0:T(1024)} %param.14) | copy-start | bytes 36868
  8.0 55.5 %all-gather.2.cloned.1.call-start = ((), (), s32[]{:S(2)}) async-start(), calls=%async_computation.1 | async-start | bytes 4177920 | tf_op jit(solution)/shard_map/all_gather | solution.py:35
  11.0 363.6 %all-reduce.3.cloned.1.call-start = ((), (), s32[]{:S(2)}) async-start(), calls=%async_computation.3 | async-start | bytes 28311552 | tf_op jit(solution)/shard_map/psum | solution.py:9
  47.3 0.7 copy-start.3
  47.3 0.7 copy-start.5
  47.3 439.2 %reduce-scatter.2.cloned.1.call-start = ((), (), s32[]{:S(2)}) async-start(), calls=%async_computation.2 | async-start | bytes 8355840 | tf_op jit(solution)/shard_map/reduce_scatter | solution.py:49
  374.6 10.2 %copy-start.4 = (bf16[768,3072]{1,0:T(8,128)(2,1)S(1)}, bf16[768,3072]{1,0:T(8,128)(2,1)}, u32[]{:S(2)}) copy-start(bf16[768,3072]{1,0:T(8,128)(2,1)} %get-tuple-element.2) | copy-start | bytes 14155780
  391.1 95.4 %copy-start.1 = (bf16[40,3072]{1,0:T(8,128)(2,1)S(1)}, bf16[40,3072]{1,0:T(8,128)(2,1)}, u32[]{:S(2)}) copy-start(bf16[40,3072]{1,0:T(8,128)(2,1)} %param.9) | copy-start | bytes 737284
  391.1 97.3 %copy-start.2 = (f32[3072]{0:T(1024)S(1)}, f32[3072]{0:T(1024)}, u32[]{:S(2)}) copy-start(f32[3072]{0:T(1024)} %param.13) | copy-start | bytes 36868
Sparse Core Ops, SparseCore 0:
  11.7 51.7 all-gather.1
  391.3 95.1 reduce-scatter.1
Sparse Core Ops, SparseCore 1:
  47.4 327.1 all-reduce.2
where the time goes:
time: 531 us; the launch traced here: 530 us
  waiting for transfers between devices  422 us (79%)
  blocking collectives  32.1 us (6%)
  local copies, waits for them, and re-layouts  24.4 us (5%)
  matrix products  18.4 us (3%)
  other arithmetic  17.2 us (3%)
  between operations  16.2 us (3%)
    psum x1, waiting for transfers between devices, spread(): return lax.psum(kept, axis)  311 us
    reduce_scatter x1, waiting for transfers between devices, per_device(): lax.psum_scatter(jnp.dot(hidden, outer_matrix, preferred_element_type=jnp...  95.3 us
    psum x1, blocking collectives, per_device(): totals = lax.psum(partial_sums, 'mp')  32.1 us
    reshape x1, local copies, waits for them, and re-layouts, per_device(): inner_matrix = inner_local.reshape(width, 2 * hidden_cols)  23.8 us
    all_gather x1, waiting for transfers between devices, per_device(): piece = lax.all_gather(normed, 'mp', axis=0, tiled=True)  15.4 us
  transfers between devices with their start and end apart: 3, of which 3 were waited for; matrix products, arithmetic and copies ran while one was open for 7% of the time, Pallas kernels for 0%

commit v1 on v0

v1 whole, which is shorter than its diff:
```python
import functools

import jax
import jax.numpy as jnp
from jax import lax
from jax.experimental import pallas as pl
from jax.experimental.pallas import tpu as pltpu
from jax.sharding import PartitionSpec as P


def spread(value, axis, source):
    kept = jnp.where(lax.axis_index(axis) == source, value, 0).astype(value.dtype)
    return lax.psum(kept, axis)


def membership(slots, lengths, offsets):
    inside = (slots[:, None] >= offsets[None, :]) & (
        slots[:, None] < offsets[None, :] + lengths[None, :]
    )
    return inside.astype(jnp.float32)


def norm_rows(tokens_f, norm_gain):
    return (
        tokens_f
        * lax.rsqrt(jnp.mean(tokens_f * tokens_f, axis=1, keepdims=True) + 1e-06)
        * norm_gain
    ).astype(jnp.bfloat16)


def finish(tokens_f, delta, final_gain, value_head, lengths, offsets):
    tok_rows = tokens_f.shape[0]
    resid = tokens_f + delta
    mixed = resid.astype(jnp.bfloat16)
    final = resid * lax.rsqrt(jnp.mean(resid * resid, axis=1, keepdims=True) + 1e-06) * final_gain
    values = jnp.dot(final, value_head, precision=lax.Precision.HIGHEST)
    own_slots = lax.axis_index("mp") * tok_rows + jnp.arange(tok_rows, dtype=jnp.int32)
    member = membership(own_slots, lengths, offsets)
    partial_sums = jnp.dot(values, member, precision=lax.Precision.HIGHEST)
    totals = lax.psum(partial_sums, "mp")
    rewards = totals / lengths.astype(jnp.float32)
    return (mixed, rewards)


def move_weights(tokens, w_in, w_down, norm_gain, final_gain, value_head, owner, lengths, offsets):
    owner_index = owner[0]
    width = tokens.shape[1]
    hidden_cols = w_in.shape[3]
    tokens_f = tokens.astype(jnp.float32)
    normed = norm_rows(tokens_f, norm_gain)
    inner_local, outer_local = (
        spread(w_in, "rep", owner_index),
        spread(w_down, "rep", owner_index),
    )
    inner_matrix = inner_local.reshape(width, 2 * hidden_cols)
    piece = lax.all_gather(normed, "mp", axis=0, tiled=True)
    slots = jnp.arange(piece.shape[0], dtype=jnp.int32)
    row_count = piece.shape[0]
    products = jnp.dot(piece, inner_matrix, preferred_element_type=jnp.float32).reshape(
        row_count, 2, hidden_cols
    )
    gate_part = products[:, 0, :]
    up_part = products[:, 1, :]
    hidden = (
        jax.nn.gelu(gate_part, approximate=True)
        * up_part
        * jnp.sum(membership(slots, lengths, offsets), axis=1)[:, None]
    ).astype(jnp.bfloat16)
    outer_matrix = outer_local.reshape(hidden_cols, width)
    delta = lax.psum_scatter(
        jnp.dot(hidden, outer_matrix, preferred_element_type=jnp.float32),
        "mp",
        scatter_dimension=0,
        tiled=True,
    )
    return finish(tokens_f, delta, final_gain, value_head, lengths, offsets)


MESH = pl.DeviceIdType.MESH


def place(half):
    rep, slot = lax.axis_index("rep"), lax.axis_index("mp")
    side, row, level = slot % 2, (slot // 2) % 2, slot // 4
    other_rep, other_row = 1 - rep, 1 - row
    first = (rep * side + other_rep * (1 - side), row * (1 - side) + other_row * side)
    second = (rep * (1 - side) + other_rep * side, row * side + other_row * (1 - side))
    return rep, slot, side, level, (rep, row), first, second, (other_rep, other_row)


def remote(src, dst, send_sem, recv_sem, column, level, side):
    return pltpu.make_async_remote_copy(
        src_ref=src, dst_ref=dst, send_sem=send_sem, recv_sem=recv_sem,
        device_id=(column[0], level * 4 + column[1] * 2 + side), device_id_type=MESH,
    )


def gather_kernel(half, own_ref, out_ref, level_send, first_send, second_send, cross_send, pass_send, recv_sem, local_sem):
    rep, slot, side, level, here, first, second, cross = place(half)
    levels = half // 2

    barrier = pltpu.get_barrier_semaphore()

    def greet(column, at, plane):
        pl.semaphore_signal(
            barrier, inc=1, device_id=(column[0], at * 4 + column[1] * 2 + plane), device_id_type=MESH
        )

    greet(first, level, side)
    greet(second, level, side)
    greet(here, level, 1 - side)

    @pl.loop(1, levels)
    def _(d):
        greet(here, (level + d) % levels, side)

    pl.semaphore_wait(barrier, levels + 2)

    def index_of(column, at):
        return (column[0] * half + at * 2 + column[1]) * 2 + side

    mine = index_of(here, level)

    def from_level(d):
        return (level + levels - d) % levels

    def climb(d):
        return remote(own_ref, out_ref.at[mine], level_send.at[d], recv_sem.at[mine], here, (level + d) % levels, side)

    def move(src, index, sem, column):
        return remote(src, out_ref.at[index], sem, recv_sem.at[index], column, level, side)

    def hand(src, index):
        return remote(src, out_ref.at[index], pass_send.at[index], recv_sem.at[index], here, level, 1 - side)

    def arrive(index):
        pltpu.make_async_copy(own_ref, out_ref.at[index], recv_sem.at[index]).wait()

    move(own_ref, mine, first_send.at[0], first).start()

    @pl.loop(1, levels)
    def _(d):
        climb(d).start()

    move(own_ref, mine, second_send.at[0], second).start()
    hand(own_ref, mine).start()
    keep = pltpu.make_async_copy(own_ref, out_ref.at[mine], local_sem)
    keep.start()

    def relay(d):
        index = index_of(first, from_level(d))
        arrive(index)
        move(out_ref.at[index], index, cross_send.at[d], second).start()
        hand(out_ref.at[index], index).start()

    def settle(d):
        for column in (second, cross):
            index = index_of(column, from_level(d))
            arrive(index)
            hand(out_ref.at[index], index).start()

    relay(0)

    @pl.loop(1, levels)
    def _(d):
        index = index_of(here, from_level(d))
        arrive(index)
        move(out_ref.at[index], index, first_send.at[d], first).start()
        move(out_ref.at[index], index, second_send.at[d], second).start()
        hand(out_ref.at[index], index).start()
        relay(d)
        settle(d - 1)

    settle(levels - 1)

    @pl.loop(0, 2 * half)
    def _(i):
        arrive(2 * i + 1 - side)

    keep.wait()

    @pl.loop(1, levels)
    def _(d):
        climb(d).wait_send()

    @pl.loop(0, levels)
    def _(d):
        for sem in (first_send, second_send, cross_send):
            move(own_ref, mine, sem.at[d], first).wait_send()

    @pl.loop(0, 2 * half)
    def _(i):
        hand(own_ref, 2 * i + side).wait_send()


def gather_rows(own, half):
    dma = pltpu.SemaphoreType.DMA
    levels = half // 2
    return pl.pallas_call(
        functools.partial(gather_kernel, half),
        out_shape=jax.ShapeDtypeStruct((4 * half,) + own.shape, own.dtype),
        in_specs=[pl.BlockSpec(memory_space=pltpu.VMEM)],
        out_specs=pl.BlockSpec(memory_space=pl.ANY),
        scratch_shapes=[
            dma((levels,)), dma((levels,)), dma((levels,)), dma((levels,)),
            dma((4 * half,)), dma((4 * half,)), dma,
        ],
        compiler_params=pltpu.CompilerParams(collective_id=0, has_side_effects=True),
    )(own)


def reduce_kernel(half, part_ref, tok_ref, live_ref, member_ref, final_ref, head_ref, mixed_ref, totals_ref,
                  swap_buf, mine_buf, sum_buf, cross_buf, first_buf, second_buf, level_buf, acc, mean_buf, own_mean,
                  swap_send, swap_recv, local_sem, send_sem, cross_recv, first_recv, second_recv, level_recv,
                  mean_send, mean_recv):
    rep, slot, side, level, here, first, second, cross = place(half)
    levels, parts = half // 2, 2 * half
    barrier = pltpu.get_barrier_semaphore()
    pl.semaphore_signal(barrier, inc=1, device_id=(1 - rep, slot), device_id_type=MESH)

    @pl.loop(1, parts)
    def _(d):
        pl.semaphore_signal(barrier, inc=1, device_id=(rep, (slot + d) % parts), device_id_type=MESH)

    pl.semaphore_wait(barrier, parts)

    def target(column, d):
        return column[0] * half + ((level + d) % levels) * 2 + column[1]

    def swap(to):
        return remote(
            part_ref.at[2 * to + 1 - side], swap_buf.at[to], swap_send.at[to], swap_recv.at[to], here, level, 1 - side
        )

    def fetch(to):
        return pltpu.make_async_copy(part_ref.at[2 * to + side], mine_buf.at[to], local_sem.at[to])

    def send(to, buf, sem, slot_at, column, at):
        return remote(sum_buf.at[to], buf.at[slot_at], send_sem.at[to], sem.at[slot_at], column, at, side)

    def arrive(buf, sem, at):
        pltpu.make_async_copy(sum_buf.at[0], buf.at[at], sem.at[at]).wait()

    def both(to):
        fetch(to).wait()
        swap(to).wait_recv()
        return mine_buf[to].astype(jnp.float32) + swap_buf[to].astype(jnp.float32)

    def start(to):
        swap(to).start()
        fetch(to).start()

    @pl.loop(1, levels + 1)
    def _(d):
        start(target(cross, d))
        start(target(second, d))

    @pl.loop(1, levels + 1)
    def _(d):
        start(target(first, d))
        start(target(here, d))

    @pl.loop(1, levels + 1)
    def _(d):
        at = (level + d) % levels
        to = target(cross, d)
        sum_buf[to] = both(to).astype(jnp.bfloat16)
        send(to, cross_buf, cross_recv, at, second, level).start()
        to = target(second, d)
        sum_buf[to] = both(to).astype(jnp.bfloat16)
        send(to, second_buf, second_recv, at, second, level).start()

    @pl.loop(1, levels + 1)
    def _(d):
        at = (level + d) % levels
        to = target(first, d)
        mine = both(to)
        arrive(cross_buf, cross_recv, at)
        sum_buf[to] = (mine + cross_buf[at].astype(jnp.float32)).astype(jnp.bfloat16)
        send(to, first_buf, first_recv, at, first, level).start()

    def collect(d):
        at = (level + d) % levels
        mine = both(target(here, d))
        arrive(second_buf, second_recv, at)
        arrive(first_buf, first_recv, at)
        return mine + (second_buf[at].astype(jnp.float32) + first_buf[at].astype(jnp.float32))

    @pl.loop(1, levels)
    def _(d):
        to = target(here, d)
        sum_buf[to] = collect(d).astype(jnp.bfloat16)
        send(to, level_buf, level_recv, level, here, (level + d) % levels).start()

    acc[...] = collect(0)

    @pl.loop(1, levels)
    def _(d):
        at = (level + levels - d) % levels
        arrive(level_buf, level_recv, at)
        acc[...] += level_buf[at].astype(jnp.float32)

    resid = tok_ref[...].astype(jnp.float32) + acc[...] * live_ref[...]
    mixed_ref[...] = resid.astype(jnp.bfloat16)
    scale = lax.rsqrt(jnp.mean(resid * resid, axis=1, keepdims=True) + 1e-06)
    values = jnp.sum(resid * scale * final_ref[...] * head_ref[...], axis=1, keepdims=True)
    own_mean[...] = jnp.broadcast_to(jnp.sum(values * member_ref[...], axis=0, keepdims=True), own_mean.shape)

    def tell(d):
        to = (slot + d) % parts
        return pltpu.make_async_remote_copy(
            src_ref=own_mean, dst_ref=mean_buf.at[slot], send_sem=mean_send.at[to],
            recv_sem=mean_recv.at[slot], device_id=(rep, to), device_id_type=MESH,
        )

    @pl.loop(1, parts)
    def _(d):
        tell(d).start()

    totals_ref[...] = own_mean[...]

    @pl.loop(1, parts)
    def _(d):
        index = (slot + parts - d) % parts
        pltpu.make_async_copy(own_mean, mean_buf.at[index], mean_recv.at[index]).wait()
        totals_ref[...] += mean_buf[index]

    @pl.loop(0, levels)
    def _(d):
        for column in (cross, second, first, here):
            swap(target(column, d)).wait_send()
        for column in (cross, second, first):
            send(target(column, d), cross_buf, cross_recv, level, second, level).wait_send()

    @pl.loop(1, levels)
    def _(d):
        send(target(here, d), level_buf, level_recv, level, second, level).wait_send()

    @pl.loop(1, parts)
    def _(d):
        tell(d).wait_send()


def reduce_rows(part, tokens, live, member, final_gain, value_head, half):
    shape = tokens.shape
    levels, chips, parts = half // 2, 2 * half, 2 * half
    vmem = pl.BlockSpec(memory_space=pltpu.VMEM)
    dma = pltpu.SemaphoreType.DMA
    block = pltpu.VMEM((chips,) + shape, jnp.bfloat16)
    few = pltpu.VMEM((levels,) + shape, jnp.bfloat16)
    return pl.pallas_call(
        functools.partial(reduce_kernel, half),
        out_shape=(
            jax.ShapeDtypeStruct(shape, jnp.bfloat16),
            jax.ShapeDtypeStruct((8, 128), jnp.float32),
        ),
        in_specs=[pl.BlockSpec(memory_space=pl.ANY)] + [vmem] * 5,
        out_specs=(vmem, vmem),
        scratch_shapes=[
            block, block, block, few, few, few, few,
            pltpu.VMEM(shape, jnp.float32),
            pltpu.VMEM((parts, 8, 128), jnp.float32),
            pltpu.VMEM((8, 128), jnp.float32),
            dma((chips,)), dma((chips,)), dma((chips,)), dma((chips,)),
            dma((levels,)), dma((levels,)), dma((levels,)), dma((levels,)),
            dma((parts,)), dma((parts,)),
        ],
        compiler_params=pltpu.CompilerParams(
            collective_id=1, has_side_effects=True, vmem_limit_bytes=48 << 20
        ),
    )(part, tokens, live, member, final_gain[None, :], value_head[None, :])


def move_rows(reps, parts, tokens, w_in, w_down, norm_gain, final_gain, value_head, owner, lengths, offsets):
    tok_rows, width = tokens.shape
    half = parts // 2
    normed = norm_rows(tokens.astype(jnp.float32), norm_gain)
    rows = gather_rows(normed, half).reshape(reps * parts * tok_rows, width)
    gate = jnp.dot(rows, w_in[0, :, 0, :], preferred_element_type=jnp.float32)
    up = jnp.dot(rows, w_in[0, :, 1, :], preferred_element_type=jnp.float32)
    mine = owner[0] == lax.axis_index("rep")
    hidden = jnp.where(mine, jax.nn.gelu(gate, approximate=True) * up, 0.0).astype(jnp.bfloat16)
    part = jnp.dot(hidden, w_down[0], preferred_element_type=jnp.float32).astype(jnp.bfloat16)
    own_slots = lax.axis_index("mp") * tok_rows + jnp.arange(tok_rows, dtype=jnp.int32)
    member = membership(own_slots, lengths, offsets)
    live = jnp.sum(member, axis=1)[:, None]
    count = lengths.shape[0]
    member = jnp.pad(member, ((0, 0), (0, 128 - count)))
    mixed, totals = reduce_rows(
        part.reshape(reps * parts, tok_rows, width), tokens, live, member, final_gain, value_head, half
    )
    return mixed, totals[0, :count] / lengths.astype(jnp.float32)


def lengths_fit(args):
    return args[7].shape[0] <= 128


def per_device(reps, parts, *args):
    tokens, w_in, w_down = args[:3]
    row_bytes = 2 * reps * parts * tokens.size * 2
    weight_bytes = 2 * (w_in.size + w_down.size)
    if reps == 2 and parts % 4 == 0 and lengths_fit(args) and row_bytes < 2 * weight_bytes:
        return move_rows(reps, parts, *args)
    return move_weights(*args)


def solution(mesh):
    in_specs = (
        P(("rep", "mp"), None),
        P("rep", None, None, "mp"),
        P("rep", "mp", None),
        P(),
        P(),
        P(),
        P("mp"),
        P("rep"),
        P("rep"),
    )
    out_specs = (P(("rep", "mp"), None), P("rep"))
    return jax.shard_map(
        functools.partial(per_device, mesh.shape["rep"], mesh.shape["mp"]),
        mesh=mesh, in_specs=in_specs, out_specs=out_specs, check_vma=False,
    )
```

time: 531 us -> 176 us (0.33)
  waiting for transfers between devices: 422 us -> 0 us
  Pallas kernels: 0 us -> 115 us
  blocking collectives: 32.1 us -> 0 us
  matrix products: 18.4 us -> 37.8 us
  other arithmetic: 17.2 us -> 1.77 us
  between operations: 16.2 us -> 1.4 us
    psum x1 -> x0, waiting for transfers between devices: 311 us -> none  [spread(): return lax.psum(kept, axis)]
    pallas_call x0 -> x2, Pallas kernels: none -> 115 us  [the longest x1 68.7 us: reduce_rows(): pl.pallas_call(functools.partial(reduce_kernel, half), out_shape=(jax.Sha...]
    reduce_scatter x1 -> x0, waiting for transfers between devices: 95.3 us -> none  [per_device(): lax.psum_scatter(jnp.dot(hidden, outer_matrix, preferred_element_type=jnp...]
    psum x1 -> x0, blocking collectives: 32.1 us -> none  [per_device(): totals = lax.psum(partial_sums, 'mp')]
    reshape x1 -> x0, local copies, waits for them, and re-layouts: 23.8 us -> none  [per_device(): inner_matrix = inner_local.reshape(width, 2 * hidden_cols)]
    dot_general x4 -> x2, matrix products: 18.4 us -> 37.8 us  [the longest x1 24.5 us: move_rows(): jnp.dot(hidden, w_down[0], preferred_element_type=jnp.float32)]
    slice x0 -> x1, local copies, waits for them, and re-layouts: none -> 19.1 us  [move_rows(): up = jnp.dot(rows, w_in[0, :, 1, :], preferred_element_type=jnp.float32)]
    all_gather x1 -> x0, waiting for transfers between devices: 15.4 us -> none  [per_device(): piece = lax.all_gather(normed, 'mp', axis=0, tiled=True)]
  transfers between devices with their start and end apart: 3 -> 0, of which waited for: 3 -> 0; matrix products, arithmetic and copies ran while one was open for 7% -> 0% of each run, Pallas kernels for 0% -> 0%
where the time goes in v1:
time: 176 us
  Pallas kernels  115 us (65%)
  matrix products  37.8 us (21%)
  local copies, waits for them, and re-layouts  19.9 us (11%)
  other arithmetic  1.77 us (1%)
    pallas_call x1, Pallas kernels, reduce_rows(): pl.pallas_call(functools.partial(reduce_kernel, half), out_shape=(jax.Sha...  68.7 us
    pallas_call x1, Pallas kernels, gather_rows(): pl.pallas_call(functools.partial(gather_kernel, half), out_shape=jax.Shap...  46 us
    dot_general x1, matrix products, move_rows(): jnp.dot(hidden, w_down[0], preferred_element_type=jnp.float32)  24.5 us
    slice x1, local copies, waits for them, and re-layouts, move_rows(): up = jnp.dot(rows, w_in[0, :, 1, :], preferred_element_type=jnp.float32)  19.1 us
    dot_general x1, matrix products, move_rows(): gate = jnp.dot(rows, w_in[0, :, 0, :], preferred_element_type=jnp.float32)  13.3 us

profile of v1, /device:TPU:0, one launch (start us, length us, event | category | flops | bytes accessed | tf_op | source)
XLA Modules:
  0.0 175.5 jit_solution(4341042654271620837)
XLA Ops:
  0.6 0.0 copy-start
  0.6 0.0 copy-start.3
  0.6 19.1 %fusion.18 = (bf16[1,3072,1,768]{3,2,1,0:T(2,128)(2,1)}, bf16[1,3072,1,768]{3,2,1,0:T(2,128)(2,1)}) fusion(bf16[1,3072,2,768]{3,2,1,0:T(2,128)(2,1)} %param.10), kind=kLoop, calls=%fused_computation.29 | loop fusion | bytes 18874368 | tf_op jit(solution)/shard_map/slice | solution.py:380
  19.7 0.0 copy-done
  19.8 0.2 fusion.13
  19.9 0.0 copy-done.3
  19.9 0.8 fusion.15.own_ref
  20.7 46.0 %shard_map.104 = bf16[32,40,3072]{2,1,0:T(8,128)(2,1)} custom-call(bf16[40,3072]{1,0:T(8,128)(2,1)} %fusion.15.own_ref), custom_call_target="tpu_custom_call" | custom-call | tf_op jit(solution)/shard_map/pallas_call | solution.py:199
  66.7 13.3 %fusion.10 = f32[1280,768]{1,0:T(8,128)} fusion(bf16[1280,3072]{1,0:T(8,128)(2,1)} %bitcast.31, bf16[1,3072,1,768]{3,2,1,0:T(2,128)(2,1)} %get-tuple-element.7), kind=kOutput, calls=%fused_computation.14 | convolution fusion | flops 6047662080 | bytes 16515072 | tf_op jit(solution)/shard_map/dot_general | solution.py:379
  80.6 0.0 copy-start.4
  80.7 0.0 copy-start.5
  80.7 0.0 copy-start.1
  80.7 0.0 copy-start.2
  80.7 24.5 %convolution_convert_fusion = bf16[1280,3072]{1,0:T(8,128)(2,1)} fusion(bf16[1,768,3072]{2,1,0:T(8,128)(2,1)} %param.11, f32[1280,768]{1,0:T(8,128)} %fusion.10, bf16[1280,3072]{1,0:T(8,128)(2,1)} %bitcast.32, bf16[1,3072,1,768]{3,2,1,0:T(2,128)(2,1)} %get-tuple-element.6, pred[]{:T(512)S(6)} %eq.3), kind=kOutput, calls=%fused_computation | convolution fusion | flops 12086476800 | bytes 29097984 | tf_op jit(solution)/shard_map/dot_general | solution.py:383
  105.2 0.0 copy-done.4
  105.2 0.0 copy-done.5
  105.2 0.1 and_convert_fusion
  105.3 0.2 fusion.16
  105.5 0.1 copy.19.live_ref
  105.6 0.0 copy-done.1
  105.6 0.0 copy-done.2
  105.6 68.7 %shard_map.105 = (bf16[40,3072]{1,0:T(8,128)(2,1)S(1)}, f32[8,128]{1,0:T(8,128)S(1)}) custom-call(bf16[32,40,3072]{2,1,0:T(8,128)(2,1)} %bitcast.30, bf16[40,3072]{1,0:T(8,128)(2,1)S(1)} %copy-done, f32[40,1]{1,0:T(8,128)S(1)} %copy.19.live_ref, f32[40,128]{1,0:T(8,128)S(1)} %pad.4.member_ref, f32[1,3072]{1,0:T(1,128)S(1)} %bitcast.28, f32[1,3072]{1,0:T(1,128)S(1)} %bitcast.29), custom_call_target="tpu_custom_call" | custom-call | tf_op jit(solution)/shard_map/pallas_call | solution.py:351
  174.3 0.5 bitcast_divide_fusion
  174.9 0.7 copy.36
  (4 shorter events, 0.0 us)
Async XLA Ops:
  0.6 19.1 %copy-start = (bf16[40,3072]{1,0:T(8,128)(2,1)S(1)}, bf16[40,3072]{1,0:T(8,128)(2,1)}, u32[]{:S(2)}) copy-start(bf16[40,3072]{1,0:T(8,128)(2,1)} %tok_ref.1) | copy-start | bytes 737284
  0.6 19.3 %copy-start.3 = (f32[3072]{0:T(1024)S(1)}, f32[3072]{0:T(1024)}, u32[]{:S(2)}) copy-start(f32[3072]{0:T(1024)} %param.12) | copy-start | bytes 36868
  80.6 24.6 %copy-start.4 = (s32[8]{0:T(128)S(1)}, s32[8]{0:T(128)}, u32[]{:S(2)}) copy-start(s32[8]{0:T(128)} %param.17) | copy-start | bytes 100
  80.7 24.5 %copy-start.5 = (s32[8]{0:T(128)S(1)}, s32[8]{0:T(128)}, u32[]{:S(2)}) copy-start(s32[8]{0:T(128)} %param.16) | copy-start | bytes 100
  80.7 24.9 %copy-start.1 = (f32[3072]{0:T(1024)S(1)}, f32[3072]{0:T(1024)}, u32[]{:S(2)}) copy-start(f32[3072]{0:T(1024)} %param.13) | copy-start | bytes 36868
  80.7 24.9 %copy-start.2 = (f32[3072]{0:T(1024)S(1)}, f32[3072]{0:T(1024)}, u32[]{:S(2)}) copy-start(f32[3072]{0:T(1024)} %param.14) | copy-start | bytes 36868

commit v2 on v1

--- a/solution.py
+++ b/solution.py
@@ -376,10 +376,12 @@
     half = parts // 2
     normed = norm_rows(tokens.astype(jnp.float32), norm_gain)
     rows = gather_rows(normed, half).reshape(reps * parts * tok_rows, width)
-    gate = jnp.dot(rows, w_in[0, :, 0, :], preferred_element_type=jnp.float32)
-    up = jnp.dot(rows, w_in[0, :, 1, :], preferred_element_type=jnp.float32)
+    cols = w_in.shape[3]
+    products = jnp.dot(rows, w_in.reshape(width, 2 * cols), preferred_element_type=jnp.float32)
+    gate, up = products[:, :cols], products[:, cols:]
     mine = owner[0] == lax.axis_index("rep")
     hidden = jnp.where(mine, jax.nn.gelu(gate, approximate=True) * up, 0.0).astype(jnp.bfloat16)
+    hidden = lax.optimization_barrier(hidden)
     part = jnp.dot(hidden, w_down[0], preferred_element_type=jnp.float32).astype(jnp.bfloat16)
     own_slots = lax.axis_index("mp") * tok_rows + jnp.arange(tok_rows, dtype=jnp.int32)
     member = membership(own_slots, lengths, offsets)

time: 176 us -> 163 us (0.926)
  local copies, waits for them, and re-layouts: 19.9 us -> 9.79 us
  matrix products: 37.8 us -> 29.3 us
  other arithmetic: 1.77 us -> 7.73 us
    slice x1 -> x0, local copies, waits for them, and re-layouts: 19.1 us -> none  [move_rows(): up = jnp.dot(rows, w_in[0, :, 1, :], preferred_element_type=jnp.float32)]
    dot_general x1, matrix products: 24.5 us -> 10.8 us  [move_rows(): jnp.dot(hidden, w_down[0], preferred_element_type=jnp.float32)]
    unnamed x13 -> x12, local copies, waits for them, and re-layouts: 0.73 us -> 9.69 us
    dot_general x1, matrix products: 13.3 us -> 18.5 us  [move_rows(): jnp.dot(rows, w_in.reshape(width, 2 * cols), preferred_element_type=jnp.f...]
    convert_element_type x0 -> x1, other arithmetic: none -> 4.07 us  [move_rows(): jnp.where(mine, jax.nn.gelu(gate, approximate=True) * up, 0.0)]
where the time goes in v2:
time: 163 us
  Pallas kernels  115 us (71%)
  matrix products  29.3 us (18%)
  local copies, waits for them, and re-layouts  9.79 us (6%)
  other arithmetic  7.73 us (5%)
    pallas_call x1, Pallas kernels, reduce_rows(): pl.pallas_call(functools.partial(reduce_kernel, half), out_shape=(jax.Sha...  68.8 us
    pallas_call x1, Pallas kernels, gather_rows(): pl.pallas_call(functools.partial(gather_kernel, half), out_shape=jax.Shap...  46 us
    dot_general x1, matrix products, move_rows(): jnp.dot(rows, w_in.reshape(width, 2 * cols), preferred_element_type=jnp.f...  18.5 us
    dot_general x1, matrix products, move_rows(): jnp.dot(hidden, w_down[0], preferred_element_type=jnp.float32)  10.8 us
    unnamed x12, local copies, waits for them, and re-layouts  9.69 us
    convert_element_type x1, other arithmetic, move_rows(): jnp.where(mine, jax.nn.gelu(gate, approximate=True) * up, 0.0)  4.07 us

profile of v2, /device:TPU:0, one launch (start us, length us, event | category | flops | bytes accessed | tf_op | source)
XLA Modules:
  0.0 163.1 jit_solution(9352128747379156161)
XLA Ops:
  0.6 1.1 fusion.11
  1.7 1.8 %fusion.13.own_ref = bf16[40,3072]{1,0:T(8,128)(2,1)} fusion(bf16[40,3072]{1,0:T(8,128)(2,1)} %tok_ref.1, f32[3072]{0:T(1024)} %param.12, f32[40]{0:T(128)S(1)} %add_rsqrt_fusion), kind=kLoop, calls=%fused_computation.17 | loop fusion | flops 491520 | bytes 503968 | tf_op jit(solution)/shard_map/convert_element_type | solution.py:28
  3.5 46.0 %shard_map.104 = bf16[32,40,3072]{2,1,0:T(8,128)(2,1)} custom-call(bf16[40,3072]{1,0:T(8,128)(2,1)} %fusion.13.own_ref), custom_call_target="tpu_custom_call" | custom-call | tf_op jit(solution)/shard_map/pallas_call | solution.py:199
  49.5 9.0 %copy.15 = bf16[384,8,2,768]{3,1,2,0:T(8,128)(2,1)} copy(bf16[384,8,2,768]{3,2,1,0:T(2,128)(2,1)} %bitcast.20) | data formatting | bytes 18874368
  58.5 18.5 %fusion.15 = f32[1280,1536]{1,0:T(8,128)} fusion(bf16[1280,3072]{1,0:T(8,128)(2,1)} %bitcast.23, bf16[3072,1536]{1,0:T(8,128)(2,1)} %bitcast.21), kind=kOutput, calls=%fused_computation.23 | convolution fusion | flops 12079595520 | bytes 25165824 | tf_op jit(solution)/shard_map/dot_general | solution.py:380
  77.7 4.1 %fusion.10 = bf16[1280,768]{1,0:T(8,128)(2,1)S(1)} fusion(f32[1280,1536]{1,0:T(8,128)} %fusion.15, pred[]{:T(512)S(6)} %eq.3), kind=kLoop, calls=%fused_computation.12 | loop fusion | flops 10813440 | bytes 9830401 | tf_op jit(solution)/shard_map/convert_element_type | solution.py:383
  81.8 0.0 copy-start.3
  81.8 0.0 copy-start.4
  81.8 0.0 copy-start
  81.8 0.0 copy-start.1
  81.8 0.0 copy-start.2
  81.8 10.8 %convolution_convert_fusion = bf16[1280,3072]{1,0:T(8,128)(2,1)} fusion(bf16[1280,768]{1,0:T(8,128)(2,1)S(1)} %fusion.10, bf16[1,768,3072]{2,1,0:T(8,128)(2,1)} %param.11), kind=kOutput, calls=%fused_computation | convolution fusion | flops 6043729920 | bytes 14548992 | tf_op jit(solution)/shard_map/dot_general | solution.py:385
  92.6 0.0 copy-done.3
  92.6 0.0 copy-done.4
  92.6 0.2 fusion.14
  92.8 0.1 copy.14.live_ref
  92.9 0.1 and_convert_fusion
  93.0 0.0 copy-done
  93.0 0.0 copy-done.1
  93.0 0.0 copy-done.2
  93.0 68.8 %shard_map.105 = (bf16[40,3072]{1,0:T(8,128)(2,1)S(1)}, f32[8,128]{1,0:T(8,128)S(1)}) custom-call(bf16[32,40,3072]{2,1,0:T(8,128)(2,1)} %bitcast.22, bf16[40,3072]{1,0:T(8,128)(2,1)S(1)} %copy-done, f32[40,1]{1,0:T(8,128)S(1)} %copy.14.live_ref, f32[40,128]{1,0:T(8,128)S(1)} %pad.4.member_ref, f32[1,3072]{1,0:T(1,128)S(1)} %bitcast.18, f32[1,3072]{1,0:T(1,128)S(1)} %bitcast.19), custom_call_target="tpu_custom_call" | custom-call | tf_op jit(solution)/shard_map/pallas_call | solution.py:351
  161.8 0.5 bitcast_divide_fusion
  162.4 0.7 copy.18
  (4 shorter events, 0.0 us)
Async XLA Ops:
  81.8 10.9 %copy-start.3 = (s32[8]{0:T(128)S(1)}, s32[8]{0:T(128)}, u32[]{:S(2)}) copy-start(s32[8]{0:T(128)} %param.17) | copy-start | bytes 100
  81.8 10.8 %copy-start.4 = (s32[8]{0:T(128)S(1)}, s32[8]{0:T(128)}, u32[]{:S(2)}) copy-start(s32[8]{0:T(128)} %param.16) | copy-start | bytes 100
  81.8 11.2 %copy-start = (bf16[40,3072]{1,0:T(8,128)(2,1)S(1)}, bf16[40,3072]{1,0:T(8,128)(2,1)}, u32[]{:S(2)}) copy-start(bf16[40,3072]{1,0:T(8,128)(2,1)} %tok_ref.1) | copy-start | bytes 737284
  81.8 11.2 %copy-start.1 = (f32[3072]{0:T(1024)S(1)}, f32[3072]{0:T(1024)}, u32[]{:S(2)}) copy-start(f32[3072]{0:T(1024)} %param.13) | copy-start | bytes 36868
  81.8 11.2 %copy-start.2 = (f32[3072]{0:T(1024)S(1)}, f32[3072]{0:T(1024)}, u32[]{:S(2)}) copy-start(f32[3072]{0:T(1024)} %param.14) | copy-start | bytes 36868
